TPU v7x, 32 devices: a whole 2x2x4 slice. The times are simulated.
32 devices in a mesh: grp: 2 (over y), seq: 4 (over z), head: 2 (over x), batch: 2 (over core).
Axes of the slice: x: 2, y: 2, z: 4, core: 2. Of those that a mesh axis runs over, the one named last changes fastest.
Arguments:
- queries: bfloat16 [64, 64, 128], P(('grp', 'batch'), 'head'), parts along dimension 0, may hold values from -8 to 8
- key_cache: bfloat16 [64, 8, 1024, 128], P(('grp', 'batch'), 'head', 'seq'), parts along dimension 0, may hold values from -5 to 5
- value_cache: bfloat16 [64, 8, 1024, 128], P(('grp', 'batch'), 'head', 'seq'), parts along dimension 0, may hold values from -5 to 5
- gate_logits: float32 [2, 64, 64], P(None, ('grp', 'batch'), 'head'), parts along dimension 1, may hold values from -6 to 6
- lengths: int32 [64], P(('grp', 'batch')), parts along dimension 0, may hold values from 256 to 1024, as said below
- chosen: int32 [64, 8, 2], P(('grp', 'batch'), 'head'), parts along dimension 0, may hold values from 0 to 7, as said below
- counts: int32 [64, 8], P(('grp', 'batch'), 'head'), parts along dimension 0, may hold values from 1 to 2, as said below
Outputs:
- output: bfloat16 [64, 64, 128], P(('grp', 'batch'), 'head'), parts along dimension 0
There are 2 independent parts, one for each index of `grp`. A program takes and returns all parts, laid end to end along the dimension named above; each array names one. Nothing has to cross between parts.
Inputs may be any that keep to these rules, and one draw needn't show every extreme that they name: `lengths`: every draw has a sequence of the full length 1024. `chosen`: for each sequence and key-value head the first counts entries are distinct blocks that start below the sequence's length, and the first entry is block 0; the entries after them are ignored. `counts`: every draw has a sequence with 2 valid entries for every key-value head.
All inputs are finite; a program needn't handle non-finite values.
Results may differ from a plain program's by a relative error of at most 0.02.
Values may be sent and summed in bfloat16 or wider, within the bound.
A program may use at most 64 MiB of HBM per device.

v0:
```python
import math
import jax
import jax.numpy as jnp
from jax import lax
from jax.sharding import PartitionSpec as P

BLOCK = 128


def combined_all(array, axis, join):
    gathered = jax.tree.map(
        lambda a, kind: lax.all_gather(a.astype(kind), axis),
        array,
        (jnp.bfloat16, jnp.bfloat16, jnp.bfloat16),
    )

    def take(source):
        return jax.tree.map(
            lambda a, own: lax.dynamic_index_in_dim(a, source, 0, False).astype(own.dtype),
            gathered,
            array,
        )

    return lax.fori_loop(
        1, lax.axis_size(axis), lambda source, state: join(state, take(source)), take(0)
    )


def softmax_terms(query_rows, key_rows, value_rows, live_mask, score_scale):
    scores = (
        jnp.einsum("pgd,pnd->pgn", query_rows, key_rows, preferred_element_type=jnp.float32)
        * score_scale
    )
    scores = jnp.where(live_mask[:, None, :], scores, -1e30)
    row_max = jnp.max(scores, axis=2)
    weights = jnp.where(live_mask[:, None, :], jnp.exp(scores - row_max[:, :, None]), 0.0)
    weight_sum = jnp.sum(weights, axis=2)
    summed = jnp.einsum(
        "pgn,pnd->pgd", weights.astype(jnp.bfloat16), value_rows, preferred_element_type=jnp.float32
    )
    return (row_max, weight_sum, summed)


def combine(first, second):
    merged = []
    for index in range(0, len(first), 3):
        row_max = jnp.maximum(first[index], second[index])
        factor_first = jnp.exp(first[index] - row_max)
        factor_second = jnp.exp(second[index] - row_max)
        merged.append(row_max)
        merged.append(first[index + 1] * factor_first + second[index + 1] * factor_second)
        merged.append(
            first[index + 2] * factor_first[:, :, None]
            + second[index + 2] * factor_second[:, :, None]
        )
    return tuple(merged)


def finish(weight_sum, summed):
    return summed / weight_sum[:, :, None]


def pool_blocks(key_rows, value_rows, pair_lengths, first_block):
    pair_count, tokens, head_width = key_rows.shape
    block_count = tokens // BLOCK
    position = first_block * BLOCK + jnp.arange(tokens, dtype=jnp.int32)
    live_mask = position[None, :] < pair_lengths[:, None]
    token_ones = live_mask.astype(jnp.bfloat16).reshape(pair_count, block_count, BLOCK)
    starts = (first_block + jnp.arange(block_count, dtype=jnp.int32)) * BLOCK
    filled = jnp.clip(pair_lengths[:, None] - starts[None, :], 0, BLOCK)
    root_fill = jnp.sqrt(jnp.maximum(filled, 1).astype(jnp.float32))[:, :, None]
    key_sums = jnp.einsum(
        "pjt,pjtd->pjd",
        token_ones,
        key_rows.reshape(pair_count, block_count, BLOCK, head_width),
        preferred_element_type=jnp.float32,
    )
    value_sums = jnp.einsum(
        "pjt,pjtd->pjd",
        token_ones,
        value_rows.reshape(pair_count, block_count, BLOCK, head_width),
        preferred_element_type=jnp.float32,
    )
    pooled_keys = (key_sums / root_fill).astype(jnp.bfloat16)
    pooled_values = (value_sums / root_fill).astype(jnp.bfloat16)
    return (live_mask, filled > 0, pooled_keys, pooled_values)


def picked_tokens(live_mask, chosen_rows, count_rows, first_block):
    pair_count, tokens = live_mask.shape
    block_count = tokens // BLOCK
    block_ids = first_block + jnp.arange(block_count, dtype=jnp.int32)
    slot_live = jnp.arange(chosen_rows.shape[1], dtype=jnp.int32)[None, :] < count_rows[:, None]
    picked = jnp.any(
        (chosen_rows[:, :, None] == block_ids[None, None, :]) & slot_live[:, :, None], axis=1
    )
    spread = jnp.broadcast_to(picked[:, :, None], (pair_count, block_count, BLOCK)).reshape(
        pair_count, tokens
    )
    return live_mask & spread


def blend_gates(compressed, selected, gate_pairs):
    mixed = gate_pairs[0][:, :, None] * compressed + gate_pairs[1][:, :, None] * selected
    return mixed.astype(jnp.bfloat16)


def on_device(queries, key_cache, value_cache, gate_logits, lengths, chosen, counts):
    batch_rows, head_count, context, head_width = key_cache.shape
    pair_count = batch_rows * head_count
    group_size = queries.shape[1] // head_count
    score_scale = 1.0 / math.sqrt(head_width)
    query_rows = queries.reshape(pair_count, group_size, head_width)
    pair_keys = key_cache.reshape(pair_count, context, head_width)
    pair_values = value_cache.reshape(pair_count, context, head_width)
    pair_lengths = jnp.broadcast_to(lengths[:, None], (batch_rows, head_count)).reshape(pair_count)
    pair_chosen = chosen.reshape(pair_count, chosen.shape[2])
    pair_counts = counts.reshape(pair_count)
    gate_pairs = jax.nn.sigmoid(gate_logits.reshape(2, pair_count, group_size))
    local_blocks = context // BLOCK
    first_block = lax.axis_index("seq") * local_blocks
    live_mask, block_live, pooled_keys, pooled_values = pool_blocks(
        pair_keys, pair_values, pair_lengths, first_block
    )
    token_mask = picked_tokens(live_mask, pair_chosen, pair_counts, first_block)
    all_keys, all_values = (
        lax.all_gather(pooled_keys, "seq", axis=1, tiled=True),
        lax.all_gather(pooled_values, "seq", axis=1, tiled=True),
    )
    all_starts = jnp.arange(all_keys.shape[1], dtype=jnp.int32) * BLOCK
    all_live = all_starts[None, :] < pair_lengths[:, None]
    s_max, s_sum, s_val = softmax_terms(query_rows, pair_keys, pair_values, token_mask, score_scale)
    merged = combined_all((s_max, s_sum, s_val), "seq", combine)
    c_max, c_sum, c_val = softmax_terms(query_rows, all_keys, all_values, all_live, score_scale)
    output = blend_gates(finish(c_sum, c_val), finish(merged[1], merged[2]), gate_pairs)
    return output.reshape(batch_rows, head_count * group_size, head_width)


def solution(mesh):
    return jax.shard_map(
        on_device,
        mesh=mesh,
        in_specs=(
            P(("grp", "batch"), "head", None),
            P(("grp", "batch"), "head", "seq", None),
            P(("grp", "batch"), "head", "seq", None),
            P(None, ("grp", "batch"), "head"),
            P(("grp", "batch")),
            P(("grp", "batch"), "head", None),
            P(("grp", "batch"), "head"),
        ),
        out_specs=P(("grp", "batch"), "head", None),
        check_vma=False,
    )
```

profile of v0, /device:TPU:0, one launch (start us, length us, event | category | flops | bytes accessed | tf_op | source)
XLA Modules:
  0.0 87.3 jit_solution(7308756827463599597)
XLA Ops:
  0.0 0.9 %copy-done = bf16[16,32,128]{2,1,0:T(8,128)(2,1)S(1)} copy-done((bf16[16,32,128]{2,1,0:T(8,128)(2,1)S(1)}, bf16[16,32,128]{2,1,0:T(8,128)(2,1)}, u32[]{:S(2)}) %copy-start) | copy-done | bytes 131096
  0.9 0.7 broadcast_in_dim.71
  1.6 0.1 lt.87
  1.7 0.1 compare_bitcast_fusion
  1.9 0.0 copy-start.3
  1.9 0.0 copy-start.2
  1.9 3.4 %fusion.17 = f32[64,2,1,128]{3,2,1,0:T(1,128)S(1)} fusion(bf16[64,2,128,128]{3,2,1,0:T(8,128)(2,1)} %bitcast.70, pred[64,2,128,1]{2,1,0,3:T(4,128)(4,1)S(1)} %compare_bitcast_fusion), kind=kOutput, calls=%fused_computation.25 | convolution fusion | flops 4194304 | bytes 4276224 | tf_op jit(solution)/shard_map/pjt,pjtd->pjd/dot_general | solution.py:78
  5.3 0.1 convert_sqrt_fusion
  5.4 3.4 %fusion.19 = f32[64,2,1,128]{3,2,1,0:T(1,128)S(1)} fusion(bf16[64,2,128,128]{3,2,1,0:T(8,128)(2,1)} %bitcast.68, pred[64,2,128,1]{2,1,0,3:T(4,128)(4,1)S(1)} %compare_bitcast_fusion), kind=kOutput, calls=%fused_computation.27 | convolution fusion | flops 4194304 | bytes 4276224 | tf_op jit(solution)/shard_map/pjt,pjtd->pjd/dot_general | solution.py:72
  8.8 0.1 fusion.24
  8.9 15.1 %all_gather.20 = bf16[64,8,128]{2,0,1:T(8,128)(2,1)S(1)} all-gather(bf16[64,2,128]{2,0,1:T(8,128)(2,1)S(1)} %get-tuple-element.207), channel_id=1, replica_groups=mesh['grp'=2,'seq'=4,'head'=2,'batch'=2] {'seq'}, dimensions={1}, use_global_device_ids=true | all-gather | bytes 163840 | tf_op jit(solution)/shard_map/all_gather | solution.py:127
  24.0 0.2 fusion.22
  24.2 0.1 copy.61
  24.3 0.1 broadcast_compare_fusion
  24.4 0.1 fusion.36
  24.4 0.1 copy.62
  24.6 0.1 copy.66
  24.7 0.1 lt.97
  24.8 0.1 copy.65
  24.9 0.1 eq.15
  25.0 0.1 and_reduce_fusion
  25.1 0.1 copy.67
  25.2 0.1 broadcast_in_dim.76
  25.3 0.1 bitcast_and_fusion
  25.4 3.5 %fusion.38 = (f32[64,8]{1,0:T(8,128)S(1)}, f32[64,8,256]{2,1,0:T(8,128)S(1)}) fusion(bf16[64,8,128]{2,1,0:T(8,128)(2,1)S(1)} %bitcast.67, bf16[64,256,128]{2,1,0:T(8,128)(2,1)} %bitcast.69, pred[64,256]{1,0:T(8,128)(4,1)S(1)} %bitcast_and_fusion), kind=kOutput, calls=%fused_computation.66 | convolution fusion | flops 33947136 | bytes 4868096 | tf_op jit(solution)/shard_map/pgd,pnd->pgn/dot_general | solution.py:31
  28.9 0.1 copy.68
  29.0 11.9 %all-gather.3 = bf16[4,64,8]{1,2,0:T(8,128)(2,1)S(1)} all-gather(bf16[1,64,8]{1,2,0:T(8,128)(2,1)S(1)} %copy.68), channel_id=2, replica_groups=mesh['grp'=2,'seq'=4,'head'=2,'batch'=2] {'seq'}, dimensions={0}, use_global_device_ids=true | all-gather | bytes 5120 | tf_op jit(solution)/shard_map/all_gather | solution.py:12
  40.9 0.3 fusion.12
  41.2 0.1 copy.69
  41.2 11.9 %all-gather.4 = bf16[4,64,8]{1,2,0:T(8,128)(2,1)S(1)} all-gather(bf16[1,64,8]{1,2,0:T(8,128)(2,1)S(1)} %copy.69), channel_id=3, replica_groups=mesh['grp'=2,'seq'=4,'head'=2,'batch'=2] {'seq'}, dimensions={0}, use_global_device_ids=true | all-gather | bytes 5120 | tf_op jit(solution)/shard_map/all_gather | solution.py:12
  53.2 2.9 %convolution_convert_fusion = bf16[64,8,128]{2,1,0:T(8,128)(2,1)S(1)} fusion(bf16[64,256,128]{2,1,0:T(8,128)(2,1)} %bitcast.71, f32[64,8,256]{2,1,0:T(8,128)S(1)} %get-tuple-element.210, f32[64,8]{1,0:T(8,128)S(1)} %get-tuple-element.209, pred[64,256]{1,0:T(8,128)(4,1)S(1)} %bitcast_and_fusion), kind=kOutput, calls=%fused_computation.15 | convolution fusion | flops 34013184 | bytes 4868096 | tf_op jit(solution)/shard_map/pgn,pnd->pgd/dot_general | solution.py:38
  56.1 15.0 %all-gather.2 = bf16[256,8,128]{2,1,0:T(8,128)(2,1)S(1)} all-gather(bf16[64,8,128]{2,1,0:T(8,128)(2,1)S(1)} %convolution_convert_fusion), channel_id=4, replica_groups=mesh['grp'=2,'seq'=4,'head'=2,'batch'=2] {'seq'}, dimensions={0}, use_global_device_ids=true | all-gather | bytes 655360 | tf_op jit(solution)/shard_map/all_gather | solution.py:12
  71.1 1.5 %while.19 = (s32[]{:T(128)}, f32[64,8]{0,1:T(8,128)S(1)}, f32[64,8]{0,1:T(8,128)S(1)}, f32[64,8,128]{2,1,0:T(8,128)S(1)}, bf16[4,64,8]{1,2,0:T(8,128)(2,1)S(1)},...) while((s32[]{:T(128)}, f32[64,8]{0,1:T(8,128)S(1)}, ...), condition=%wide.region_6.7_spmd, body=%wide.region_5.6_spmd.sunk | while | flops 266245 | bytes 682135 | solution.py:24
  71.2 0.1 copy.88
  71.3 0.1 copy.89
  71.3 0.3 fusion.49
  71.7 0.1 copy.88
  71.8 0.1 copy.89
  71.8 0.3 fusion.49
  72.2 0.1 copy.88
  72.2 0.1 copy.89
  72.3 0.3 fusion.49
  72.6 13.3 %all_gather.21 = bf16[64,8,128]{2,0,1:T(8,128)(2,1)S(1)} all-gather(bf16[64,2,128]{2,0,1:T(8,128)(2,1)S(1)} %get-tuple-element.206), channel_id=1, replica_groups=mesh['grp'=2,'seq'=4,'head'=2,'batch'=2] {'seq'}, dimensions={1}, use_global_device_ids=true | all-gather | bytes 163840 | tf_op jit(solution)/shard_map/all_gather | solution.py:128
  86.0 0.1 copy.70
  86.1 0.1 mul.134
  86.2 0.1 copy.64
  86.2 0.1 mul.125
  86.3 1.0 %fusion.7 = bf16[64,8,128]{2,1,0:T(8,128)(2,1)} fusion(bf16[64,8,8]{2,1,0:T(8,128)(2,1)S(1)} %copy.62, f32[64,8,128]{2,1,0:T(8,128)S(1)} %get-tuple-element.182, bf16[64,8,128]{2,0,1:T(8,128)(2,1)S(1)} %all_gather.21, f32[64,8]{1,0:T(8,128)S(1)} %copy.70, f32[64,8]{1,0:T(8,128)S(1)} %mul.134, f32[64,8]{1,0:T(8,128)S(1)} %copy.64, f32[64,8]{1,0:T(8,128)S(1)} %mul.125), kind=kOutput, calls=%fused_computation.14 | convolution fusion | flops 1441792 | bytes 540672 | tf_op jit(solution)/shard_map/pgn,pnd->pgd/dot_general | solution.py:38
  (19 shorter events, 0.1 us)
Async XLA Ops:
  0.0 0.9 %copy-start = (bf16[16,32,128]{2,1,0:T(8,128)(2,1)S(1)}, bf16[16,32,128]{2,1,0:T(8,128)(2,1)}, u32[]{:S(2)}) copy-start(bf16[16,32,128]{2,1,0:T(8,128)(2,1)} %param.9) | copy-start | bytes 393220
  1.9 22.7 %copy-start.3 = (s32[16,4]{0,1:T(4,128)S(1)}, s32[16,4]{0,1:T(4,128)}, u32[]{:S(2)}) copy-start(s32[16,4]{0,1:T(4,128)} %param.15) | copy-start | bytes 772
  1.9 22.9 %copy-start.2 = (s32[16,4,2]{0,2,1:T(2,128)S(1)}, s32[16,4,2]{0,2,1:T(2,128)}, u32[]{:S(2)}) copy-start(s32[16,4,2]{0,2,1:T(2,128)} %param.14) | copy-start | bytes 1540
  53.2 32.9 %copy-start.1 = (f32[2,16,32]{2,1,0:T(8,128)S(1)}, f32[2,16,32]{2,1,0:T(8,128)}, u32[]{:S(2)}) copy-start(f32[2,16,32]{2,1,0:T(8,128)} %param.12) | copy-start | bytes 12292
where the time goes:
time: 87.6 us; the launch traced here: 87.3 us
  blocking collectives  67.3 us (77%)
  matrix products  14.3 us (16%)
  local copies, waits for them, and re-layouts  3.58 us (4%)
  other arithmetic  1.83 us (2%)
    all_gather x3, blocking collectives, combined_all(): lax.all_gather(a.astype(kind), axis)  38.9 us
    all_gather x1, blocking collectives, on_device(): lax.all_gather(pooled_keys, 'seq', axis=1, tiled=True)  15.1 us
    all_gather x1, blocking collectives, on_device(): lax.all_gather(pooled_values, 'seq', axis=1, tiled=True)  13.3 us
    dot_general x2, matrix products, softmax_terms(): jnp.einsum('pgn,pnd->pgd', weights.astype(jnp.bfloat16), value_rows, pref...  3.93 us
    dot_general x2, matrix products, softmax_terms(): jnp.einsum('pgd,pnd->pgn', query_rows, key_rows, preferred_element_type=j...  3.65 us
    dot_general x1, matrix products, pool_blocks(): jnp.einsum('pjt,pjtd->pjd', token_ones, key_rows.reshape(pair_count, bloc...  3.39 us
    dot_general x1, matrix products, pool_blocks(): jnp.einsum('pjt,pjtd->pjd', token_ones, value_rows.reshape(pair_count, bl...  3.38 us

commit v1 on v0

--- a/solution.py
+++ b/solution.py
@@ -5,6 +5,10 @@
 from jax.sharding import PartitionSpec as P
 
 BLOCK = 128
+
+
+def link_stocks_in(target, mesh_name, axis_no):
+    return jnp.concatenate(jax.lax.all_gather(target, mesh_name), axis=axis_no)
 
 
 def combined_all(array, axis, join):
@@ -125,7 +129,7 @@
     token_mask = picked_tokens(live_mask, pair_chosen, pair_counts, first_block)
     all_keys, all_values = (
         lax.all_gather(pooled_keys, "seq", axis=1, tiled=True),
-        lax.all_gather(pooled_values, "seq", axis=1, tiled=True),
+        link_stocks_in(pooled_values, "seq", 1),
     )
     all_starts = jnp.arange(all_keys.shape[1], dtype=jnp.int32) * BLOCK
     all_live = all_starts[None, :] < pair_lengths[:, None]

time: 87.6 us -> 85 us (0.970)
  matrix products: 14.3 us -> 10.3 us
  blocking collectives: 67.3 us -> 68.3 us
    all_gather x3, blocking collectives: 38.9 us -> 41.6 us  [combined_all(): lax.all_gather(a.astype(kind), axis)]
    dot_general x1, matrix products: 3.39 us -> 1.2 us  [pool_blocks(): jnp.einsum('pjt,pjtd->pjd', token_ones, key_rows.reshape(pair_count, bloc...]
    dot_general x2, matrix products: 3.93 us -> 1.74 us  [softmax_terms(): jnp.einsum('pgn,pnd->pgd', weights.astype(jnp.bfloat16), value_rows, pref...]
    all_gather x1, blocking collectives: 15.1 us -> 13.3 us  [on_device(): lax.all_gather(pooled_keys, 'seq', axis=1, tiled=True)]
where the time goes in v1:
time: 85 us; the launch traced here: 84.8 us
  blocking collectives  68.3 us (80%)
  matrix products  10.3 us (12%)
  local copies, waits for them, and re-layouts  4.19 us (5%)
  other arithmetic  1.82 us (2%)
    all_gather x3, blocking collectives, combined_all(): lax.all_gather(a.astype(kind), axis)  41.6 us
    all_gather x1, blocking collectives, on_device(): lax.all_gather(pooled_keys, 'seq', axis=1, tiled=True)  13.3 us
    all_gather x1, blocking collectives, link_stocks_in(): return jnp.concatenate(jax.lax.all_gather(target, mesh_name), axis=axis_no)  13.3 us
    dot_general x2, matrix products, softmax_terms(): jnp.einsum('pgd,pnd->pgn', query_rows, key_rows, preferred_element_type=j...  3.8 us
    dot_general x1, matrix products, pool_blocks(): jnp.einsum('pjt,pjtd->pjd', token_ones, value_rows.reshape(pair_count, bl...  3.53 us
    dot_general x2, matrix products, softmax_terms(): jnp.einsum('pgn,pnd->pgd', weights.astype(jnp.bfloat16), value_rows, pref...  1.74 us

profile of v1, /device:TPU:0, one launch (start us, length us, event | category | flops | bytes accessed | tf_op | source)
XLA Modules:
  0.0 84.8 jit_solution(8849865567421725002)
XLA Ops:
  0.0 0.0 copy-start
  0.0 0.8 broadcast_in_dim.71
  0.8 0.1 lt.87
  0.9 0.8 copy.71
  1.6 0.1 eq.15
  1.7 0.8 copy.72
  2.5 0.1 lt.97
  2.6 0.1 and_reduce_fusion
  2.7 0.1 copy.73
  2.8 0.1 broadcast_in_dim.76
  2.9 0.0 copy-start.1
  3.0 0.1 bitcast_and_fusion
  3.1 3.6 %fusion.37 = (f32[64,8]{1,0:T(8,128)S(1)}, f32[64,8,256]{2,1,0:T(8,128)S(1)}) fusion(bf16[64,8,128]{2,1,0:T(8,128)(2,1)S(1)} %bitcast.72, bf16[64,256,128]{2,1,0:T(8,128)(2,1)} %bitcast.75, pred[64,256]{1,0:T(8,128)(4,1)S(1)} %bitcast_and_fusion), kind=kOutput, calls=%fused_computation.65 | convolution fusion | flops 33947136 | bytes 4868096 | tf_op jit(solution)/shard_map/pgd,pnd->pgn/dot_general | solution.py:35
  6.7 0.7 convolution_convert_fusion
  7.4 17.4 %all-gather.3 = bf16[256,8,128]{2,1,0:T(8,128)(2,1)S(1)} all-gather(bf16[64,8,128]{2,1,0:T(8,128)(2,1)S(1)} %convolution_convert_fusion), channel_id=5, replica_groups=mesh['grp'=2,'seq'=4,'head'=2,'batch'=2] {'seq'}, dimensions={0}, use_global_device_ids=true | all-gather | bytes 655360 | tf_op jit(solution)/shard_map/all_gather | solution.py:16
  24.8 0.3 fusion.12
  25.1 0.1 copy.75
  25.1 12.3 %all-gather.5 = bf16[4,64,8]{1,2,0:T(8,128)(2,1)S(1)} all-gather(bf16[1,64,8]{1,2,0:T(8,128)(2,1)S(1)} %copy.75), channel_id=4, replica_groups=mesh['grp'=2,'seq'=4,'head'=2,'batch'=2] {'seq'}, dimensions={0}, use_global_device_ids=true | all-gather | bytes 5120 | tf_op jit(solution)/shard_map/all_gather | solution.py:16
  37.4 0.1 copy.74
  37.5 11.9 %all-gather.4 = bf16[4,64,8]{1,2,0:T(8,128)(2,1)S(1)} all-gather(bf16[1,64,8]{1,2,0:T(8,128)(2,1)S(1)} %copy.74), channel_id=3, replica_groups=mesh['grp'=2,'seq'=4,'head'=2,'batch'=2] {'seq'}, dimensions={0}, use_global_device_ids=true | all-gather | bytes 5120 | tf_op jit(solution)/shard_map/all_gather | solution.py:16
  49.4 1.5 %while.19 = (s32[]{:T(128)}, f32[64,8]{0,1:T(8,128)S(1)}, f32[64,8]{0,1:T(8,128)S(1)}, f32[64,8,128]{2,1,0:T(8,128)S(1)}, bf16[4,64,8]{1,2,0:T(8,128)(2,1)S(1)},...) while((s32[]{:T(128)}, f32[64,8]{0,1:T(8,128)S(1)}, ...), condition=%wide.region_6.7_spmd, body=%wide.region_5.6_spmd.sunk | while | flops 266245 | bytes 682135 | solution.py:28
  49.4 0.1 copy.92
  49.5 0.1 copy.93
  49.6 0.3 fusion.49
  49.9 0.1 copy.92
  50.0 0.1 copy.93
  50.1 0.3 fusion.49
  50.4 0.1 copy.92
  50.5 0.1 copy.93
  50.6 0.3 fusion.49
  50.9 0.1 copy.76
  51.0 0.1 compare_bitcast_fusion
  51.1 3.5 %fusion.17 = f32[64,2,1,128]{3,2,1,0:T(1,128)S(1)} fusion(bf16[64,2,128,128]{3,2,1,0:T(8,128)(2,1)} %bitcast.73, pred[64,2,128,1]{2,1,0,3:T(4,128)(4,1)S(1)} %compare_bitcast_fusion), kind=kOutput, calls=%fused_computation.25 | convolution fusion | flops 4194304 | bytes 4276224 | tf_op jit(solution)/shard_map/pjt,pjtd->pjd/dot_general | solution.py:82
  54.6 1.2 %fusion.19 = f32[64,2,1,128]{3,2,1,0:T(1,128)S(1)} fusion(bf16[64,2,128,128]{3,2,1,0:T(8,128)(2,1)S(1)} %bitcast.76, pred[64,2,128,1]{2,1,0,3:T(4,128)(4,1)S(1)} %compare_bitcast_fusion), kind=kOutput, calls=%fused_computation.27 | convolution fusion | flops 4194304 | bytes 4276224 | tf_op jit(solution)/shard_map/pjt,pjtd->pjd/dot_general | solution.py:76
  55.8 0.1 convert_sqrt_fusion
  55.9 0.1 fusion.23
  56.0 13.3 %all_gather.23 = bf16[64,8,128]{2,0,1:T(8,128)(2,1)S(1)} all-gather(bf16[64,2,128]{2,0,1:T(8,128)(2,1)S(1)} %get-tuple-element.207), channel_id=1, replica_groups=mesh['grp'=2,'seq'=4,'head'=2,'batch'=2] {'seq'}, dimensions={1}, use_global_device_ids=true | all-gather | bytes 163840 | tf_op jit(solution)/shard_map/all_gather | solution.py:131
  69.4 0.2 fusion.21
  69.6 0.1 copy.66
  69.7 0.1 broadcast_compare_fusion
  69.8 0.1 fusion.35
  69.9 0.1 copy.69
  70.0 0.1 copy.70
  70.1 13.3 %all-gather = bf16[256,2,128]{2,1,0:T(2,128)(2,1)S(1)} all-gather(bf16[64,2,128]{2,1,0:T(2,128)(2,1)S(1)} %copy.67), channel_id=2, replica_groups=mesh['grp'=2,'seq'=4,'head'=2,'batch'=2] {'seq'}, dimensions={0}, use_global_device_ids=true | all-gather | bytes 163840 | tf_op jit(solution)/shard_map/all_gather | solution.py:11
  83.5 0.1 copy.68
  83.6 0.1 mul.125
  83.7 0.1 mul.134
  83.8 1.0 %fusion.7 = bf16[64,8,128]{2,1,0:T(8,128)(2,1)} fusion(bf16[64,8,8]{2,1,0:T(8,128)(2,1)S(1)} %copy.69, bf16[64,8,128]{2,1,0:T(8,128)(2,1)S(1)} %bitcast.80, f32[64,8,128]{2,1,0:T(8,128)S(1)} %get-tuple-element.182, f32[64,8]{1,0:T(8,128)S(1)} %copy.76, f32[64,8]{1,0:T(8,128)S(1)} %mul.134, f32[64,8]{1,0:T(8,128)S(1)} %copy.70, f32[64,8]{1,0:T(8,128)S(1)} %mul.125), kind=kOutput, calls=%fused_computation.14 | convolution fusion | flops 1441792 | bytes 540672 | tf_op jit(solution)/shard_map/pgn,pnd->pgd/dot_general | solution.py:42
  (21 shorter events, 0.2 us)
Async XLA Ops:
  0.0 3.1 %copy-start = (bf16[16,32,128]{2,1,0:T(8,128)(2,1)S(1)}, bf16[16,32,128]{2,1,0:T(8,128)(2,1)}, u32[]{:S(2)}) copy-start(bf16[16,32,128]{2,1,0:T(8,128)(2,1)} %param.9) | copy-start | bytes 393220
  2.9 3.7 %copy-start.1 = (bf16[16,4,256,128]{3,2,1,0:T(8,128)(2,1)S(1)}, bf16[16,4,256,128]{3,2,1,0:T(8,128)(2,1)}, u32[]{:S(2)}) copy-start(bf16[16,4,256,128]{3,2,1,0:T(8,128)(2,1)} %param.11) | copy-start | bytes 12582916
  51.0 3.7 %copy-start.2 = (bf16[16,4,256,128]{3,2,1,0:T(8,128)(2,1)S(1)}, bf16[16,4,256,128]{3,2,1,0:T(8,128)(2,1)}, u32[]{:S(2)}) copy-start(bf16[16,4,256,128]{3,2,1,0:T(8,128)(2,1)} %param.10) | copy-start | bytes 12582916
  54.6 28.9 %copy-start.3 = (f32[2,16,32]{2,1,0:T(8,128)S(1)}, f32[2,16,32]{2,1,0:T(8,128)}, u32[]{:S(2)}) copy-start(f32[2,16,32]{2,1,0:T(8,128)} %param.12) | copy-start | bytes 12292
